TPU v7x, 32 devices: a whole 2x2x4 slice. The times are simulated.
32 devices in a mesh: var: 8 (over z, core), samp: 4 (over y, x).
Axes of the slice: x: 2, y: 2, z: 4, core: 2. Of those that a mesh axis runs over, the one named last changes fastest.
Arguments:
- geno: bfloat16 [8192, 16384], P('samp', 'var'), may hold values from -5 to 5
- scale_index: int32 [64, 16384], P('samp', 'var'), may hold values from 0 to 15
- scale_table: float32 [16], replicated, may hold values from 0.25 to 4
- residual: float32 [8, 8192], P(None, 'samp'), may hold values from -6 to 6
- beta_active: float32 [8, 3584], P(None, 'var'), may hold values from -6 to 6
- block_inverse: float32 [16, 256, 256], P('var'), may hold values from -1 to 4
- active_ids: int32 [3584], P('var'), may hold values from 0 to 16383, as said below
- admit_ids: int32 [512], P('var'), may hold values from 0 to 16383, as said below
Outputs:
- scores: float32 [8, 16384], P(None, 'var')
- coefficients: float32 [8, 4096], P(None, 'var')
- residual_out: float32 [8, 8192], P(None, 'samp')
Inputs may be any that keep to these rules, and one draw needn't show every extreme that they name: Variant ids, all different from one another and from those of admit_ids. The fitting slots of one index of var are its 448 entries of active_ids followed by its 64 entries of admit_ids; of these 512 slots at most 128 name variants held by any one index of var, and for every index of var some one holder reaches exactly 128. `admit_ids`: variant ids, as for active_ids.
All inputs are finite; a program needn't handle non-finite values.
Results may differ from a plain program's by a relative error of at most 0.004.
Values may be sent and summed in bfloat16 or wider, within the bound.
A program may use at most 128 MiB of HBM per device.

v0:
```python
import math
import jax
import jax.numpy as jnp
from jax import lax
from jax.sharding import PartitionSpec as P

PASSES = 3
penalty = 0.5
epsilon = 1e-06


def dequantize(values, indices, lookup):
    levels = lookup.shape[0]
    onehot = (indices[:, :, None] == jnp.arange(levels, dtype=jnp.int32)).astype(jnp.float32)
    scales = jnp.dot(onehot, lookup, precision=lax.Precision.HIGHEST)
    groups = indices.shape[0]
    widened = (
        values.reshape(groups, values.shape[0] // groups, values.shape[1]).astype(jnp.float32)
        * scales[:, None, :]
    )
    return widened.reshape(values.shape).astype(jnp.bfloat16)


def slot_layout(variant_ids, var_width, var_count):
    holder = variant_ids // var_width
    column = variant_ids % var_width
    owner_marks = (holder[..., None] == jnp.arange(var_count, dtype=jnp.int32)).astype(jnp.int32)
    before = jnp.cumsum(owner_marks, axis=-2) - owner_marks
    serial = jnp.sum(before * owner_marks, -1)
    return (holder, column, serial)


def block_update(gradient, coeffs, inverse):
    phenos, fit_width = gradient.shape
    blocks, block_size = (inverse.shape[0], inverse.shape[1])
    inner_term = (gradient - penalty * coeffs).reshape(phenos, blocks, block_size)
    direction = jnp.einsum("bij,pbj->pbi", inverse, inner_term, precision=lax.Precision.HIGHEST)
    return direction.reshape(phenos, fit_width).astype(jnp.bfloat16)


def on_device(
    geno, scale_index, scale_table, residual, beta_active, block_inverse, active_ids, admit_ids
):
    var_count = lax.axis_size("var")
    var_rank = lax.axis_index("var")
    samp_rows, var_width = geno.shape
    inv_root = 1.0 / math.sqrt(samp_rows * lax.axis_size("samp"))
    phenos = residual.shape[0]
    local_ids = jnp.concatenate([active_ids, admit_ids])
    fit_width = local_ids.shape[0]
    capacity = 2 * fit_width // var_count
    dequant = dequantize(geno, scale_index, scale_table)
    resid_low = residual.astype(jnp.bfloat16)
    screened = (
        lax.psum(jnp.dot(resid_low, dequant, preferred_element_type=jnp.float32), "samp") * inv_root
    )
    all_ids = lax.all_gather(local_ids, "var", axis=0, tiled=True).reshape(var_count, fit_width)
    holder, column, serial = slot_layout(all_ids, var_width, var_count)
    held_here = holder == var_rank
    wanted = held_here[:, None, :] & (
        serial[:, None, :] == jnp.arange(capacity, dtype=jnp.int32)[None, :, None]
    )
    source_column = jnp.sum(jnp.where(wanted, column[:, None, :], 0), -1).reshape(-1)
    present = jnp.any(wanted, -1).reshape(-1)
    selected = jnp.where(
        present[None, :], jnp.take(dequant, source_column, axis=1), jnp.zeros((), jnp.bfloat16)
    )
    position = lax.dynamic_index_in_dim(holder * capacity + serial, var_rank, 0, keepdims=False)
    coeffs = jnp.concatenate([beta_active, jnp.zeros((phenos, admit_ids.shape[0]), jnp.float32)], 1)
    current = residual
    for pass_index in range(PASSES):
        partial_sums = lax.psum(
            jnp.dot(resid_low, selected, preferred_element_type=jnp.float32), "samp"
        )
        routed = lax.all_to_all(partial_sums, "var", split_axis=1, concat_axis=1, tiled=True)
        gradient = jnp.take(routed, position, axis=1) * inv_root
        direction = block_update(gradient, coeffs, block_inverse)
        placed = (
            jnp.zeros((phenos, var_count * capacity), jnp.bfloat16).at[:, position].set(direction)
        )
        returned = lax.all_to_all(placed, "var", split_axis=1, concat_axis=1, tiled=True)
        partial_update = jnp.einsum(
            "pc,sc->ps", returned, selected, preferred_element_type=jnp.float32
        )
        update = lax.psum(partial_update, "var") * inv_root
        cross_sum, square = lax.psum(
            (jnp.sum(current * update, 1), jnp.sum(update * update, 1)), "samp"
        )
        factor = (cross_sum / (square + epsilon))[:, None]
        current = current - factor * update
        coeffs = coeffs + factor * direction.astype(jnp.float32)
        if pass_index + 1 < PASSES:
            resid_low = current.astype(jnp.bfloat16)
    return (screened, coeffs, current)


def solution(mesh):
    placed = (
        P("samp", "var"),
        P("samp", "var"),
        P(),
        P(None, "samp"),
        P(None, "var"),
        P("var", None, None),
        P("var"),
        P("var"),
    )
    return jax.shard_map(
        on_device,
        mesh=mesh,
        in_specs=placed,
        out_specs=(P(None, "var"), P(None, "var"), P(None, "samp")),
        check_vma=False,
    )
```

profile of v0, /device:TPU:0, one launch (start us, length us, event | category | flops | bytes accessed | tf_op | source)
XLA Modules:
  0.0 450.3 jit_solution(15364064158792349478)
XLA Ops:
  10.1 12.3 %copy.78 = bf16[2048,2048]{0,1:T(8,128)(2,1)} copy(bf16[2048,2048]{1,0:T(8,128)(2,1)} %param.10) | data formatting | bytes 16777216 | tf_op args[0]
  22.5 14.5 %all-gather = s32[8,1,512]{2,1,0:T(1,128)S(1)} all-gather(s32[1,1,512]{2,1,0:T(1,128)S(1)} %bitcast.157), channel_id=1, replica_groups=mesh['var'=8,'samp'=4] {'var'}, dimensions={0}, use_global_device_ids=true | all-gather | bytes 18432 | tf_op jit(solution)/shard_map/all_gather | solution.py:57
  37.0 9.0 %reduce-window.6 = s32[8,8,4,128]{3,1,2,0:T(8,128)S(1)} reduce-window(s32[8,8,4,128]{3,1,2,0:T(8,128)S(1)} %fusion.13, s32[]{:T(128)} %constant.73.clone.1), window={size=1x1x1x128 pad=0_0x0_0x0_0x127_0}, to_apply=%region_1.2 | reduce-window | flops 4161536 | bytes 262148 | tf_op jit(solution)/shard_map/reduce-window
  47.6 4.6 %mul.124 = f32[16,128,2048]{1,0,2:T(8,128)S(1)} broadcast(f32[16,2048]{0,1:T(8,128)S(1)} %bitcast.133), dimensions={0,2} | broadcast | bytes 16908288 | tf_op jit(solution)/shard_map/mul | solution.py:18
  52.2 9.2 %fusion = bf16[2048,2048]{0,1:T(8,128)(2,1)} fusion(f32[256,8,16,128]{3,2,1,0:T(8,128)S(1)} %bitcast.130, bf16[2048,2048]{0,1:T(8,128)(2,1)S(1)} %bitcast.132), kind=kLoop, calls=%fused_computation.8 | loop fusion | flops 12582912 | bytes 33554432 | tf_op jit(solution)/shard_map/convert_element_type | solution.py:21
  61.4 13.3 %gather_fusion = bf16[1024,2048]{1,0:T(8,128)(2,1)} fusion(bf16[2048,2048]{0,1:T(8,128)(2,1)} %fusion, s32[1024]{0:T(1024)S(1)} %broadcast_clamp_fusion), kind=kCustom, calls=%fused_computation.3 | custom fusion | bytes 8392704 | tf_op jit(solution)/shard_map/jit(_take)/gather | solution.py:66
  74.7 2.8 select_select_fusion
  77.5 2.0 copy-done.1
  80.6 16.9 %psum.92 = f32[8,8,128]{2,0,1:T(8,128)} all-reduce(f32[8,8,128]{2,0,1:T(8,128)S(1)} %convolution_bitcast_fusion.3), channel_id=1, replica_groups=mesh['var'=8,'samp'=4] {'samp'}, use_global_device_ids=true, to_apply=%region_6.7 | all-reduce | flops 8192 | bytes 65536 | tf_op jit(solution)/shard_map/psum | solution.py:72
  97.5 3.4 all-to-all-start
  101.2 5.5 %all-to-all-done = f32[8,8,128]{2,0,1:T(8,128)S(1)} async-done(((f32[8,8,128]{2,0,1:T(8,128)}), f32[8,8,128]{2,0,1:T(8,128)S(1)}, u32[]{:S(2)}, u32[]{:S(2)}) %all-to-all-start) | async-done | bytes 32800 | tf_op jit(solution)/shard_map/all_to_all | solution.py:75
  108.7 1.8 scatter_custom_fusion
  110.7 8.0 %all_to_all.72 = bf16[8,8,128]{2,0,1:T(8,128)(2,1)S(1)} all-to-all(bf16[8,8,128]{2,0,1:T(8,128)(2,1)S(1)} %copy.84), channel_id=1, replica_groups=mesh['var'=8,'samp'=4] {'var'}, dimensions={1} | all-to-all | bytes 32768 | tf_op jit(solution)/shard_map/all_to_all | solution.py:81
  118.7 3.5 fusion.24
  122.2 51.3 %all-reduce.11.cloned.1.call-done = f32[8,2048]{1,0:T(8,128)} async-done(((f32[8,2048]{1,0:T(8,128)}), f32[8,2048]{1,0:T(8,128)}) %all-reduce.11.cloned.1.call-update) | async-done | bytes 65552 | tf_op jit(solution)/shard_map/psum | solution.py:85
  174.5 9.8 %all-reduce.3 = (f32[8]{0:T(128)S(1)}, f32[8]{0:T(128)S(1)}) all-reduce(f32[8]{0:T(128)S(1)} %get-tuple-element.21, f32[8]{0:T(128)S(1)} %get-tuple-element.20), channel_id=1, replica_groups=mesh['var'=8,'samp'=4] {'samp'}, use_global_device_ids=true, to_apply=%region_10.12 | all-reduce | flops 16 | bytes 128 | tf_op jit(solution)/shard_map/psum | solution.py:86
  185.3 3.4 convolution_bitcast_fusion.2
  188.7 14.4 %psum.96 = f32[8,8,128]{2,0,1:T(8,128)S(1)} all-reduce(f32[8,8,128]{2,0,1:T(8,128)S(1)} %convolution_bitcast_fusion.2), channel_id=1, replica_groups=mesh['var'=8,'samp'=4] {'samp'}, use_global_device_ids=true, to_apply=%region_13.15 | all-reduce | flops 8192 | bytes 65536 | tf_op jit(solution)/shard_map/psum | solution.py:72
  203.0 8.3 %all_to_all.73 = f32[8,8,128]{2,0,1:T(8,128)S(1)} all-to-all(f32[8,8,128]{2,0,1:T(8,128)S(1)} %psum.96), channel_id=1, replica_groups=mesh['var'=8,'samp'=4] {'var'}, dimensions={1} | all-to-all | bytes 65536 | tf_op jit(solution)/shard_map/all_to_all | solution.py:75
  215.4 8.0 %all_to_all.74 = bf16[8,8,128]{2,0,1:T(8,128)(2,1)S(1)} all-to-all(bf16[8,8,128]{2,0,1:T(8,128)(2,1)S(1)} %copy.88), channel_id=1, replica_groups=mesh['var'=8,'samp'=4] {'var'}, dimensions={1} | all-to-all | bytes 32768 | tf_op jit(solution)/shard_map/all_to_all | solution.py:81
  223.4 3.5 fusion.21
  226.9 52.2 %all-reduce.13.cloned.1.call-done = f32[8,2048]{1,0:T(8,128)} async-done(((f32[8,2048]{1,0:T(8,128)}), f32[8,2048]{1,0:T(8,128)}) %all-reduce.13.cloned.1.call-update) | async-done | bytes 65552 | tf_op jit(solution)/shard_map/psum | solution.py:85
  280.1 9.8 %all-reduce.2 = (f32[8]{0:T(128)S(1)}, f32[8]{0:T(128)S(1)}) all-reduce(f32[8]{0:T(128)S(1)} %get-tuple-element.19, f32[8]{0:T(128)S(1)} %get-tuple-element.18), channel_id=1, replica_groups=mesh['var'=8,'samp'=4] {'samp'}, use_global_device_ids=true, to_apply=%region_17.19 | all-reduce | flops 16 | bytes 128 | tf_op jit(solution)/shard_map/psum | solution.py:86
  290.9 3.4 convolution_bitcast_fusion.1
  294.3 14.4 %psum.100 = f32[8,8,128]{2,0,1:T(8,128)S(1)} all-reduce(f32[8,8,128]{2,0,1:T(8,128)S(1)} %convolution_bitcast_fusion.1), channel_id=1, replica_groups=mesh['var'=8,'samp'=4] {'samp'}, use_global_device_ids=true, to_apply=%region_20.22 | all-reduce | flops 8192 | bytes 65536 | tf_op jit(solution)/shard_map/psum | solution.py:72
  308.6 8.3 %all_to_all.75 = f32[8,8,128]{2,0,1:T(8,128)S(1)} all-to-all(f32[8,8,128]{2,0,1:T(8,128)S(1)} %psum.100), channel_id=1, replica_groups=mesh['var'=8,'samp'=4] {'var'}, dimensions={1} | all-to-all | bytes 65536 | tf_op jit(solution)/shard_map/all_to_all | solution.py:75
  321.6 3.3 all-to-all-start.5
  325.2 6.3 %convolution_bitcast_fusion = f32[8,2048]{1,0:T(8,128)} fusion(bf16[2048,2048]{0,1:T(8,128)(2,1)} %fusion, f32[8,2048]{1,0:T(8,128)S(1)} %copy-done.2), kind=kOutput, calls=%fused_computation.10 | convolution fusion | flops 67125248 | bytes 8519680 | tf_op jit(solution)/shard_map/dot_general | solution.py:55
  331.6 3.5 fusion.18
  335.1 38.0 %all-reduce.9.cloned.1.call-done = f32[8,2048]{1,0:T(8,128)} async-done(((f32[8,2048]{1,0:T(8,128)}), f32[8,2048]{1,0:T(8,128)}) %all-reduce.9.cloned.1.call-update) | async-done | bytes 65552 | tf_op jit(solution)/shard_map/psum | solution.py:55
  374.6 55.2 %all-reduce.15.cloned.1.call-done = f32[8,2048]{1,0:T(8,128)} async-done(((f32[8,2048]{1,0:T(8,128)}), f32[8,2048]{1,0:T(8,128)}) %all-reduce.15.cloned.1.call-update) | async-done | bytes 65552 | tf_op jit(solution)/shard_map/psum | solution.py:85
  430.8 9.8 %all-reduce.1 = (f32[8]{0:T(128)S(1)}, f32[8]{0:T(128)S(1)}) all-reduce(f32[8]{0:T(128)S(1)} %get-tuple-element.17, f32[8]{0:T(128)S(1)} %get-tuple-element.16), channel_id=1, replica_groups=mesh['var'=8,'samp'=4] {'samp'}, use_global_device_ids=true, to_apply=%region_24.26 | all-reduce | flops 16 | bytes 128 | tf_op jit(solution)/shard_map/psum | solution.py:86
  (82 shorter events, 24.9 us)
Async XLA Ops:
  8.0 100.0 %copy-start = (f32[2,256,256]{2,1,0:T(8,128)S(1)}, f32[2,256,256]{2,1,0:T(8,128)}, u32[]{:S(2)}) copy-start(f32[2,256,256]{2,1,0:T(8,128)} %param.15) | copy-start | bytes 1572868
  10.0 12.4 %copy-start.4 = (s32[448]{0:T(512)S(1)}, s32[448]{0:T(512)}, u32[]{:S(2)}) copy-start(s32[448]{0:T(512)} %param.16) | copy-start | bytes 5380
  10.0 12.3 %copy-start.5 = (s32[64]{0:T(128)S(1)}, s32[64]{0:T(128)}, u32[]{:S(2)}) copy-start(s32[64]{0:T(128)} %param.17) | copy-start | bytes 772
  46.5 5.7 %slice-start = ((s8[8388608]{0:T(1024)(128)(4,1)}), s8[4194304]{0:T(1024)(128)(4,1)S(1)}, s32[]{:S(2)}) async-start(s8[8388608]{0:T(1024)(128)(4,1)} %bitcast.131), calls=%async_computation.10 | async-start | bytes 8388608
  47.6 4.6 %slice-start.1 = ((s8[8388608]{0:T(1024)(128)(4,1)}), s8[4194304]{0:T(1024)(128)(4,1)S(1)}, s32[]{:S(2)}) async-start(s8[8388608]{0:T(1024)(128)(4,1)} %bitcast.131), calls=%async_computation.11 | async-start | bytes 8388608
  74.7 4.8 %copy-start.2 = (f32[8,2048]{1,0:T(8,128)S(1)}, f32[8,2048]{1,0:T(8,128)}, u32[]{:S(2)}) copy-start(f32[8,2048]{1,0:T(8,128)} %param.13) | copy-start | bytes 196612
  77.5 2.0 copy-start.1
  79.5 28.5 %copy-start.3 = (f32[8,448]{1,0:T(8,128)S(1)}, f32[8,448]{1,0:T(8,128)}, u32[]{:S(2)}) copy-start(f32[8,448]{1,0:T(8,128)} %param.14) | copy-start | bytes 43012
  97.5 9.1 %all-to-all-start = ((f32[8,8,128]{2,0,1:T(8,128)}), f32[8,8,128]{2,0,1:T(8,128)S(1)}, u32[]{:S(2)}, u32[]{:S(2)}) async-start(f32[8,8,128]{2,0,1:T(8,128)} %psum.92), calls=%async_computation | async-start | bytes 65536 | tf_op jit(solution)/shard_map/all_to_all | solution.py:75
  100.9 72.6 %all-reduce.11.cloned.1.call-start = ((), (), s32[]{:S(2)}) async-start(), calls=%async_computation.7 | async-start | bytes 131072 | tf_op jit(solution)/shard_map/psum | solution.py:85
  122.2 156.9 %all-reduce.13.cloned.1.call-start = ((), (), s32[]{:S(2)}) async-start(), calls=%async_computation.8 | async-start | bytes 131072 | tf_op jit(solution)/shard_map/psum | solution.py:85
  321.6 10.0 %all-to-all-start.5 = ((bf16[8,8,128]{2,0,1:T(8,128)(2,1)}), bf16[8,8,128]{2,0,1:T(8,128)(2,1)S(1)}, u32[]{:S(2)}, u32[]{:S(2)}) async-start(bf16[8,8,128]{2,0,1:T(8,128)(2,1)} %copy.92), calls=%async_computation.5 | async-start | bytes 32768 | tf_op jit(solution)/shard_map/all_to_all | solution.py:81
  325.0 48.1 %all-reduce.9.cloned.1.call-start = ((), (), s32[]{:S(2)}) async-start(), calls=%async_computation.6 | async-start | bytes 131072 | tf_op jit(solution)/shard_map/psum | solution.py:55
  331.5 98.2 %all-reduce.15.cloned.1.call-start = ((), (), s32[]{:S(2)}) async-start(), calls=%async_computation.9 | async-start | bytes 131072 | tf_op jit(solution)/shard_map/psum | solution.py:85
Sparse Core Ops, SparseCore 0:
  122.3 51.1 all-reduce.10
  227.1 52.0 all-reduce.12
Sparse Core Ops, SparseCore 1:
  331.6 41.4 all-reduce.8
  375.3 54.4 all-reduce.14
where the time goes:
time: 452 us; the launch traced here: 450 us
  waiting for transfers between devices  202 us (45%)
  blocking collectives  122 us (27%)
  local copies, waits for them, and re-layouts  43.8 us (10%)
  other arithmetic  31 us (7%)
  matrix products  27.8 us (6%)
  between operations  15.9 us (4%)
  starting transfers between devices  7.27 us (2%)
    psum x3, waiting for transfers between devices, on_device(): update = lax.psum(partial_update, 'var') * inv_root  159 us
    psum x3, blocking collectives, on_device(): lax.psum(jnp.dot(resid_low, selected, preferred_element_type=jnp.float32)...  45.6 us
    psum x1, waiting for transfers between devices, on_device(): lax.psum(jnp.dot(resid_low, dequant, preferred_element_type=jnp.float32),...  38 us
    psum x3, blocking collectives, on_device(): lax.psum((jnp.sum(current * update, 1), jnp.sum(update * update, 1)), 'sa...  29.5 us
    all_to_all x2, blocking collectives, on_device(): lax.all_to_all(partial_sums, 'var', split_axis=1, concat_axis=1, tiled=True)  16.6 us
    all_to_all x2, blocking collectives, on_device(): lax.all_to_all(placed, 'var', split_axis=1, concat_axis=1, tiled=True)  16 us
    all_gather x1, blocking collectives, on_device(): lax.all_gather(local_ids, 'var', axis=0, tiled=True)  14.5 us
    unnamed x17, local copies, waits for them, and re-layouts  14.3 us
  transfers between devices with their start and end apart: 6, of which 5 were waited for; matrix products, arithmetic and copies ran while one was open for 2% of the time, Pallas kernels for 0%

commit v1 on v0

--- a/solution.py
+++ b/solution.py
@@ -72,7 +72,12 @@
         partial_sums = lax.psum(
             jnp.dot(resid_low, selected, preferred_element_type=jnp.float32), "samp"
         )
-        routed = lax.all_to_all(partial_sums, "var", split_axis=1, concat_axis=1, tiled=True)
+        routed = jnp.concatenate(
+            lax.all_to_all(
+                jnp.stack(jnp.split(partial_sums, lax.axis_size("var"), axis=1)), "var", 0, 0
+            ),
+            axis=1,
+        )
         gradient = jnp.take(routed, position, axis=1) * inv_root
         direction = block_update(gradient, coeffs, block_inverse)
         placed = (

time: 452 us -> 456 us (level)
  local copies, waits for them, and re-layouts: 43.8 us -> 48.6 us
    unnamed x17 -> x38, local copies, waits for them, and re-layouts: 14.3 us -> 18.5 us
where the time goes in v1:
time: 456 us; the launch traced here: 455 us
  waiting for transfers between devices  202 us (44%)
  blocking collectives  122 us (27%)
  local copies, waits for them, and re-layouts  48.6 us (11%)
  other arithmetic  31 us (7%)
  matrix products  27.8 us (6%)
  between operations  16 us (4%)
  starting transfers between devices  7.27 us (2%)
    psum x3, waiting for transfers between devices, on_device(): update = lax.psum(partial_update, 'var') * inv_root  159 us
    psum x3, blocking collectives, on_device(): lax.psum(jnp.dot(resid_low, selected, preferred_element_type=jnp.float32)...  45 us
    psum x1, waiting for transfers between devices, on_device(): lax.psum(jnp.dot(resid_low, dequant, preferred_element_type=jnp.float32),...  38 us
    psum x3, blocking collectives, on_device(): lax.psum((jnp.sum(current * update, 1), jnp.sum(update * update, 1)), 'sa...  29.5 us
    unnamed x38, local copies, waits for them, and re-layouts  18.5 us
    all_to_all x2, blocking collectives, on_device(): lax.all_to_all(jnp.stack(jnp.split(partial_sums, lax.axis_size('var'), ax...  16.6 us
    all_to_all x2, blocking collectives, on_device(): lax.all_to_all(placed, 'var', split_axis=1, concat_axis=1, tiled=True)  16 us
    all_gather x1, blocking collectives, on_device(): lax.all_gather(local_ids, 'var', axis=0, tiled=True)  14.5 us
  transfers between devices with their start and end apart: 6, of which 5 were waited for; matrix products, arithmetic and copies ran while one was open for 2% of the time, Pallas kernels for 0%

profile of v1, /device:TPU:0, one launch (start us, length us, event | category | flops | bytes accessed | tf_op | source)
XLA Modules:
  0.0 454.7 jit_solution(18445301802834207062)
XLA Ops:
  10.1 12.3 %copy.75 = bf16[2048,2048]{0,1:T(8,128)(2,1)} copy(bf16[2048,2048]{1,0:T(8,128)(2,1)} %param.10) | data formatting | bytes 16777216 | tf_op args[0]
  22.5 14.5 %all-gather = s32[8,1,512]{2,1,0:T(1,128)S(1)} all-gather(s32[1,1,512]{2,1,0:T(1,128)S(1)} %bitcast.253), channel_id=1, replica_groups=mesh['var'=8,'samp'=4] {'var'}, dimensions={0}, use_global_device_ids=true | all-gather | bytes 18432 | tf_op jit(solution)/shard_map/all_gather | solution.py:57
  37.0 9.0 %reduce-window.6 = s32[8,8,4,128]{3,1,2,0:T(8,128)S(1)} reduce-window(s32[8,8,4,128]{3,1,2,0:T(8,128)S(1)} %fusion.13, s32[]{:T(128)} %constant.73.clone.1), window={size=1x1x1x128 pad=0_0x0_0x0_0x127_0}, to_apply=%region_1.2 | reduce-window | flops 4161536 | bytes 262148 | tf_op jit(solution)/shard_map/reduce-window
  47.6 4.6 %mul.124 = f32[16,128,2048]{1,0,2:T(8,128)S(1)} broadcast(f32[16,2048]{0,1:T(8,128)S(1)} %bitcast.229), dimensions={0,2} | broadcast | bytes 16908288 | tf_op jit(solution)/shard_map/mul | solution.py:18
  52.2 9.2 %fusion = bf16[2048,2048]{0,1:T(8,128)(2,1)} fusion(f32[256,8,16,128]{3,2,1,0:T(8,128)S(1)} %bitcast.226, bf16[2048,2048]{0,1:T(8,128)(2,1)S(1)} %bitcast.228), kind=kLoop, calls=%fused_computation.8 | loop fusion | flops 12582912 | bytes 33554432 | tf_op jit(solution)/shard_map/convert_element_type | solution.py:21
  61.4 13.3 %gather_fusion = bf16[1024,2048]{1,0:T(8,128)(2,1)} fusion(bf16[2048,2048]{0,1:T(8,128)(2,1)} %fusion, s32[1024]{0:T(1024)S(1)} %broadcast_clamp_fusion), kind=kCustom, calls=%fused_computation.3 | custom fusion | bytes 8392704 | tf_op jit(solution)/shard_map/jit(_take)/gather | solution.py:66
  74.7 2.8 select_select_fusion
  77.5 2.0 copy-done.1
  80.6 16.3 %psum.92 = f32[8,1024]{1,0:T(8,128)S(1)} all-reduce(f32[8,1024]{1,0:T(8,128)S(1)} %convolution_bitcast_fusion.1), channel_id=1, replica_groups=mesh['var'=8,'samp'=4] {'samp'}, use_global_device_ids=true, to_apply=%region_6.7 | all-reduce | flops 8192 | bytes 65536 | tf_op jit(solution)/shard_map/psum | solution.py:72
  101.7 3.4 all-to-all-start
  105.4 5.5 %all-to-all-done = f32[8,8,128]{2,1,0:T(8,128)S(1)} async-done(((f32[8,8,128]{2,1,0:T(8,128)}), f32[8,8,128]{2,1,0:T(8,128)S(1)}, u32[]{:S(2)}, u32[]{:S(2)}) %all-to-all-start) | async-done | bytes 32800 | tf_op jit(solution)/shard_map/all_to_all | solution.py:76
  112.9 1.8 scatter_custom_fusion
  114.8 8.0 %all_to_all.51 = bf16[8,8,128]{2,0,1:T(8,128)(2,1)S(1)} all-to-all(bf16[8,8,128]{2,0,1:T(8,128)(2,1)S(1)} %copy.81), channel_id=1, replica_groups=mesh['var'=8,'samp'=4] {'var'}, dimensions={1} | all-to-all | bytes 32768 | tf_op jit(solution)/shard_map/all_to_all | solution.py:86
  122.9 3.5 fusion.26
  126.4 51.3 %all-reduce.11.cloned.1.call-done = f32[8,2048]{1,0:T(8,128)} async-done(((f32[8,2048]{1,0:T(8,128)}), f32[8,2048]{1,0:T(8,128)}) %all-reduce.11.cloned.1.call-update) | async-done | bytes 65552 | tf_op jit(solution)/shard_map/psum | solution.py:90
  178.7 9.8 %all-reduce.3 = (f32[8]{0:T(128)S(1)}, f32[8]{0:T(128)S(1)}) all-reduce(f32[8]{0:T(128)S(1)} %get-tuple-element.21, f32[8]{0:T(128)S(1)} %get-tuple-element.20), channel_id=1, replica_groups=mesh['var'=8,'samp'=4] {'samp'}, use_global_device_ids=true, to_apply=%region_10.12 | all-reduce | flops 16 | bytes 128 | tf_op jit(solution)/shard_map/psum | solution.py:91
  189.5 3.4 fusion.16
  192.8 14.4 %psum.96 = f32[8,1024]{1,0:T(8,128)S(1)} all-reduce(f32[8,1024]{1,0:T(8,128)S(1)} %fusion.16), channel_id=1, replica_groups=mesh['var'=8,'samp'=4] {'samp'}, use_global_device_ids=true, to_apply=%region_13.15 | all-reduce | flops 8192 | bytes 65536 | tf_op jit(solution)/shard_map/psum | solution.py:72
  207.3 8.3 %all_to_all.52 = f32[8,8,128]{2,1,0:T(8,128)S(1)} all-to-all(f32[8,8,128]{2,1,0:T(8,128)S(1)} %constant_dynamic-update-slice_fusion.8), channel_id=1, replica_groups=mesh['var'=8,'samp'=4] {'var'}, dimensions={0} | all-to-all | bytes 65536 | tf_op jit(solution)/shard_map/all_to_all | solution.py:76
  219.7 8.0 %all_to_all.53 = bf16[8,8,128]{2,0,1:T(8,128)(2,1)S(1)} all-to-all(bf16[8,8,128]{2,0,1:T(8,128)(2,1)S(1)} %copy.85), channel_id=1, replica_groups=mesh['var'=8,'samp'=4] {'var'}, dimensions={1} | all-to-all | bytes 32768 | tf_op jit(solution)/shard_map/all_to_all | solution.py:86
  227.7 3.5 fusion.23
  231.2 52.2 %all-reduce.13.cloned.1.call-done = f32[8,2048]{1,0:T(8,128)} async-done(((f32[8,2048]{1,0:T(8,128)}), f32[8,2048]{1,0:T(8,128)}) %all-reduce.13.cloned.1.call-update) | async-done | bytes 65552 | tf_op jit(solution)/shard_map/psum | solution.py:90
  284.4 9.8 %all-reduce.2 = (f32[8]{0:T(128)S(1)}, f32[8]{0:T(128)S(1)}) all-reduce(f32[8]{0:T(128)S(1)} %get-tuple-element.19, f32[8]{0:T(128)S(1)} %get-tuple-element.18), channel_id=1, replica_groups=mesh['var'=8,'samp'=4] {'samp'}, use_global_device_ids=true, to_apply=%region_17.19 | all-reduce | flops 16 | bytes 128 | tf_op jit(solution)/shard_map/psum | solution.py:91
  295.1 3.4 fusion.14
  298.5 14.4 %psum.100 = f32[8,1024]{1,0:T(8,128)S(1)} all-reduce(f32[8,1024]{1,0:T(8,128)S(1)} %fusion.14), channel_id=1, replica_groups=mesh['var'=8,'samp'=4] {'samp'}, use_global_device_ids=true, to_apply=%region_20.22 | all-reduce | flops 8192 | bytes 65536 | tf_op jit(solution)/shard_map/psum | solution.py:72
  313.0 8.3 %all_to_all.54 = f32[8,8,128]{2,1,0:T(8,128)S(1)} all-to-all(f32[8,8,128]{2,1,0:T(8,128)S(1)} %constant_dynamic-update-slice_fusion.16), channel_id=1, replica_groups=mesh['var'=8,'samp'=4] {'var'}, dimensions={0} | all-to-all | bytes 65536 | tf_op jit(solution)/shard_map/all_to_all | solution.py:76
  326.0 3.3 all-to-all-start.5
  329.6 6.3 %convolution_bitcast_fusion = f32[8,2048]{1,0:T(8,128)} fusion(bf16[2048,2048]{0,1:T(8,128)(2,1)} %fusion, f32[8,2048]{1,0:T(8,128)S(1)} %copy-done.2), kind=kOutput, calls=%fused_computation.10 | convolution fusion | flops 67125248 | bytes 8519680 | tf_op jit(solution)/shard_map/dot_general | solution.py:55
  335.9 3.5 fusion.20
  339.4 38.0 %all-reduce.9.cloned.1.call-done = f32[8,2048]{1,0:T(8,128)} async-done(((f32[8,2048]{1,0:T(8,128)}), f32[8,2048]{1,0:T(8,128)}) %all-reduce.9.cloned.1.call-update) | async-done | bytes 65552 | tf_op jit(solution)/shard_map/psum | solution.py:55
  378.9 55.2 %all-reduce.15.cloned.1.call-done = f32[8,2048]{1,0:T(8,128)} async-done(((f32[8,2048]{1,0:T(8,128)}), f32[8,2048]{1,0:T(8,128)}) %all-reduce.15.cloned.1.call-update) | async-done | bytes 65552 | tf_op jit(solution)/shard_map/psum | solution.py:90
  435.2 9.8 %all-reduce.1 = (f32[8]{0:T(128)S(1)}, f32[8]{0:T(128)S(1)}) all-reduce(f32[8]{0:T(128)S(1)} %get-tuple-element.17, f32[8]{0:T(128)S(1)} %get-tuple-element.16), channel_id=1, replica_groups=mesh['var'=8,'samp'=4] {'samp'}, use_global_device_ids=true, to_apply=%region_24.26 | all-reduce | flops 16 | bytes 128 | tf_op jit(solution)/shard_map/psum | solution.py:91
  (106 shorter events, 29.7 us)
Async XLA Ops:
  8.0 104.2 %copy-start = (f32[2,256,256]{2,1,0:T(8,128)S(1)}, f32[2,256,256]{2,1,0:T(8,128)}, u32[]{:S(2)}) copy-start(f32[2,256,256]{2,1,0:T(8,128)} %param.15) | copy-start | bytes 1572868
  10.0 12.4 %copy-start.4 = (s32[448]{0:T(512)S(1)}, s32[448]{0:T(512)}, u32[]{:S(2)}) copy-start(s32[448]{0:T(512)} %param.16) | copy-start | bytes 5380
  10.0 12.3 %copy-start.5 = (s32[64]{0:T(128)S(1)}, s32[64]{0:T(128)}, u32[]{:S(2)}) copy-start(s32[64]{0:T(128)} %param.17) | copy-start | bytes 772
  46.5 5.7 %slice-start = ((s8[8388608]{0:T(1024)(128)(4,1)}), s8[4194304]{0:T(1024)(128)(4,1)S(1)}, s32[]{:S(2)}) async-start(s8[8388608]{0:T(1024)(128)(4,1)} %bitcast.227), calls=%async_computation.10 | async-start | bytes 8388608
  47.6 4.6 %slice-start.1 = ((s8[8388608]{0:T(1024)(128)(4,1)}), s8[4194304]{0:T(1024)(128)(4,1)S(1)}, s32[]{:S(2)}) async-start(s8[8388608]{0:T(1024)(128)(4,1)} %bitcast.227), calls=%async_computation.11 | async-start | bytes 8388608
  74.7 4.8 %copy-start.2 = (f32[8,2048]{1,0:T(8,128)S(1)}, f32[8,2048]{1,0:T(8,128)}, u32[]{:S(2)}) copy-start(f32[8,2048]{1,0:T(8,128)} %param.13) | copy-start | bytes 196612
  77.5 2.0 copy-start.1
  79.5 32.7 %copy-start.3 = (f32[8,448]{1,0:T(8,128)S(1)}, f32[8,448]{1,0:T(8,128)}, u32[]{:S(2)}) copy-start(f32[8,448]{1,0:T(8,128)} %param.14) | copy-start | bytes 43012
  101.7 9.1 %all-to-all-start = ((f32[8,8,128]{2,1,0:T(8,128)}), f32[8,8,128]{2,1,0:T(8,128)S(1)}, u32[]{:S(2)}, u32[]{:S(2)}) async-start(f32[8,8,128]{2,1,0:T(8,128)} %constant_dynamic-update-slice_fusion), calls=%async_computation | async-start | bytes 65536 | tf_op jit(solution)/shard_map/all_to_all | solution.py:76
  105.1 72.6 %all-reduce.11.cloned.1.call-start = ((), (), s32[]{:S(2)}) async-start(), calls=%async_computation.7 | async-start | bytes 131072 | tf_op jit(solution)/shard_map/psum | solution.py:90
  126.4 157.0 %all-reduce.13.cloned.1.call-start = ((), (), s32[]{:S(2)}) async-start(), calls=%async_computation.8 | async-start | bytes 131072 | tf_op jit(solution)/shard_map/psum | solution.py:90
  326.0 10.0 %all-to-all-start.5 = ((bf16[8,8,128]{2,0,1:T(8,128)(2,1)}), bf16[8,8,128]{2,0,1:T(8,128)(2,1)S(1)}, u32[]{:S(2)}, u32[]{:S(2)}) async-start(bf16[8,8,128]{2,0,1:T(8,128)(2,1)} %copy.89), calls=%async_computation.5 | async-start | bytes 32768 | tf_op jit(solution)/shard_map/all_to_all | solution.py:86
  329.3 48.2 %all-reduce.9.cloned.1.call-start = ((), (), s32[]{:S(2)}) async-start(), calls=%async_computation.6 | async-start | bytes 131072 | tf_op jit(solution)/shard_map/psum | solution.py:55
  335.9 98.3 %all-reduce.15.cloned.1.call-start = ((), (), s32[]{:S(2)}) async-start(), calls=%async_computation.9 | async-start | bytes 131072 | tf_op jit(solution)/shard_map/psum | solution.py:90
Sparse Core Ops, SparseCore 0:
  126.5 51.1 all-reduce.10
  231.3 52.0 all-reduce.12
Sparse Core Ops, SparseCore 1:
  336.0 41.4 all-reduce.8
  379.6 54.4 all-reduce.14
